TPU v7x, 256 devices: a whole 4x4x8 slice. The times are simulated.
256 devices in a mesh: dp: 32 (over z_hi, y, core), tensor: 8 (over z_lo, x).
Axes of the slice: x: 4, y: 4, z: 8 (z_hi: 4, z_lo: 2; z = z_hi * 2 + z_lo), core: 2. Of those that a mesh axis runs over, the one named last changes fastest.
Arguments:
- tokens: bfloat16 [8192, 2560], P('dp'), may hold values from -6 to 6
- target: bfloat16 [8192, 2560], P('dp'), may hold values from -6 to 6
- norm_gain: float32 [2560], replicated, may hold values from 0.25 to 1.75
- gate_weight: bfloat16 [2560, 7168], P('dp', 'tensor'), may hold values from -0.125 to 0.125
- up_weight: bfloat16 [2560, 7168], P('dp', 'tensor'), may hold values from -0.125 to 0.125
- down_weight: bfloat16 [7168, 2560], P('tensor', 'dp'), may hold values from -0.0625 to 0.0625
- tangent: bfloat16 [2560, 7168], P('dp', 'tensor'), may hold values from -0.125 to 0.125
- lengths: int32 [4], replicated, may hold values from 512 to 2048
- loss_scale: float32 [1], replicated, may hold values from 16 to 64
Outputs:
- hvp: float32 [2560, 7168], P('dp', 'tensor')
- rayleigh: float32 [1], replicated
All inputs are finite; a program needn't handle non-finite values.
Results may differ from a plain program's by a relative error of at most 0.017.
Values may be sent and summed in bfloat16 or wider, within the bound.
No kernel may reach another device: no remote copies, remote signals or barrier semaphores. Data moves between devices by JAX's collectives and lax.ppermute only.
A program may use at most 128 MiB of HBM per device.

v0:
```python
import jax
import jax.numpy as jnp
from jax import lax
from jax.sharding import Mesh
from jax.sharding import PartitionSpec as P

DP = ("dp_0", "dp_1", "dp_2")
TENSOR = ("tensor_0", "tensor_1")
DP_TENSOR = ("dp_0", "dp_1", "dp_2", "tensor_0", "tensor_1")


def in_one_piece(arrays, axis, dim, along):
    both = jnp.concatenate(arrays, axis=along)
    filled, at, outs = (lax.all_gather(both, axis, axis=dim, tiled=True), 0, [])
    for a in arrays:
        outs.append(lax.slice_in_dim(filled, at, at + a.shape[along], axis=along))
        at += a.shape[along]
    return tuple(outs)


def one_axis_at_a_time(value, axes):
    for axis in axes:
        value = lax.psum(value, axis)
    return value


def token_weights(first_pos, row_total, micro_len, lengths, loss_scale):
    position = first_pos + jnp.arange(row_total, dtype=jnp.int32)
    micro_id = position // micro_len
    offset = position - micro_id * micro_len
    onehot = micro_id[:, None] == jnp.arange(lengths.shape[0], dtype=jnp.int32)[None, :]
    live_len = jnp.sum(jnp.where(onehot, lengths[None, :], 0), axis=1)
    return jnp.where(
        offset < live_len, loss_scale[0] / live_len.astype(jnp.float32), jnp.float32(0.0)
    )


def shards(
    tokens, target, norm_gain, gate_weight, up_weight, down_weight, tangent, lengths, loss_scale
):
    row_count = tokens.shape[0]
    stream = tokens.astype(jnp.float32)
    mean_sq = jnp.mean(stream * stream, axis=-1, keepdims=True)
    normed = (stream * lax.rsqrt(mean_sq + 1e-06) * norm_gain[None, :]).astype(jnp.bfloat16)
    pieces = in_one_piece((gate_weight, up_weight, tangent), DP, 0, 1)
    columns = normed
    gate_pre, up_pre, gate_tan = tuple(
        (jnp.dot(columns, piece, preferred_element_type=jnp.float32) for piece in pieces)
    )
    sigma = jax.nn.sigmoid(gate_pre)
    slope = sigma * (1.0 + gate_pre * (1.0 - sigma))
    bend = sigma * (1.0 - sigma) * (2.0 + gate_pre * (1.0 - 2.0 * sigma))
    hidden = (gate_pre * sigma * up_pre).astype(jnp.bfloat16)
    hidden_tan = (slope * gate_tan * up_pre).astype(jnp.bfloat16)
    down_full = lax.all_gather(down_weight, DP, axis=1, tiled=True)
    stacked = jnp.dot(
        jnp.concatenate([hidden, hidden_tan], axis=0), down_full, preferred_element_type=jnp.float32
    )
    branch = stacked[:row_count]
    branch_tan = stacked[row_count:]
    micro_len = row_count * lax.axis_size(DP) // lengths.shape[0]
    first_row = lax.axis_index(DP) * row_count
    branch, branch_tan = (
        lax.psum(branch.astype(jnp.bfloat16), TENSOR).astype(jnp.float32),
        lax.psum(branch_tan.astype(jnp.bfloat16), TENSOR).astype(jnp.float32),
    )
    weight = token_weights(first_row, row_count, micro_len, lengths, loss_scale)
    output = stream + branch
    grad_out = (weight[:, None] * (output - target.astype(jnp.float32))).astype(jnp.bfloat16)
    grad_tan = (weight[:, None] * branch_tan).astype(jnp.bfloat16)
    grads = lax.dot_general(
        jnp.concatenate([grad_out, grad_tan], axis=0),
        down_full,
        (((1,), (1,)), ((), ())),
        preferred_element_type=jnp.float32,
    )
    grad_hid = grads[:row_count]
    hess_hid = grads[row_count:]
    hess_pre = (hess_hid * up_pre * slope + grad_hid * up_pre * bend * gate_tan).astype(
        jnp.bfloat16
    )
    tangent_f = tangent.astype(jnp.float32)
    tangent_sq = jnp.sum(tangent_f * tangent_f)
    curvature, squares = (
        one_axis_at_a_time(jnp.sum(gate_tan * hess_pre.astype(jnp.float32)), DP_TENSOR),
        one_axis_at_a_time(tangent_sq, DP_TENSOR),
    )
    columns = normed
    product = lax.dot_general(
        columns, hess_pre, (((0,), (0,)), ((), ())), preferred_element_type=jnp.float32
    )
    hvp = lax.psum_scatter(
        lax.optimization_barrier(product.astype(jnp.bfloat16))
        .astype(jnp.float32)
        .astype(jnp.bfloat16),
        DP,
        scatter_dimension=0,
        tiled=True,
    ).astype(jnp.float32)
    rayleigh = (curvature / squares).reshape(1)
    return (hvp, rayleigh)


def solution(mesh):
    torus = Mesh(
        mesh.devices.reshape(4, 4, 2, 2, 4), ("dp_0", "dp_1", "dp_2", "tensor_0", "tensor_1")
    )
    return jax.shard_map(
        shards,
        mesh=torus,
        in_specs=(
            P(DP, None),
            P(DP, None),
            P(),
            P(DP, TENSOR),
            P(DP, TENSOR),
            P(TENSOR, DP),
            P(DP, TENSOR),
            P(),
            P(),
        ),
        out_specs=(P(DP, TENSOR), P()),
        check_vma=False,
    )
```

profile of v0, /device:TPU:2, one launch (start us, length us, event | category | flops | bytes accessed | tf_op | source)
XLA Modules:
  0.0 400.0 jit_solution(3529880794193507350)
XLA Ops:
  7.2 0.0 copy-start
  7.2 0.0 copy-start.7
  7.2 0.0 all-gather.3.cloned.1.call-start
  7.2 1.9 pad_maximum_fusion
  9.2 0.0 all-gather.3.cloned.1.call-update
  9.2 0.0 all-gather.5.cloned.1.call-start
  9.2 0.7 all-gather.5.cloned.1.call-update
  9.9 0.0 all-reduce.8.cloned.1.call-start
  10.0 1.7 fusion.6
  11.7 97.1 %all-gather.3.cloned.1.call-done = bf16[2560,2688]{1,0:T(8,128)(2,1)} async-done(((bf16[80,2688]{1,0:T(8,128)(2,1)}), bf16[2560,2688]{1,0:T(8,128)(2,1)}) %all-gather.3.cloned.1.call-update) | async-done | bytes 13762576 | tf_op jit(solution)/shard_map/all_gather | solution.py:14
  108.7 0.0 copy-done
  108.7 0.0 copy-done.7
  108.7 3.9 fusion
  112.6 3.9 fusion.4
  116.5 0.0 copy-start.2
  116.5 0.9 copy-done.2
  117.4 5.0 %multiply_convert_fusion.2 = (bf16[256,896]{1,0:T(8,128)(2,1)S(1)}, bf16[256,896]{1,0:T(8,128)(2,1)S(1)}, f32[256,896]{1,0:T(8,128)}) fusion(f32[256,896]{1,0:T(8,128)S(1)} %fusion.4, f32[256,896]{1,0:T(8,128)S(1)} %fusion, bf16[2560,2688]{1,0:T(8,128)(2,1)} %all-gather.3.cloned.1.call-done, bf16[256,2560]{1,0:T(8,128)(2,1)S(1)} %copy-done, ...), kind=kOutput, calls=%fused_computation.39 | convolution fusion | flops 1180008448 | bytes 9579520 | tf_op jit(solution)/shard_map/dot_general | solution.py:48
  122.4 58.1 %all-gather.5.cloned.1.call-done = bf16[896,2560]{0,1:T(8,128)(2,1)} async-done(((bf16[896,80]{0,1:T(8,128)(2,1)}), bf16[896,2560]{0,1:T(8,128)(2,1)}) %all-gather.5.cloned.1.call-update) | async-done | bytes 4587536 | tf_op jit(solution)/shard_map/all_gather | solution.py:55
  180.5 5.8 %convolution_convert_fusion.1 = bf16[512,2560]{1,0:T(8,128)(2,1)S(1)} fusion(bf16[896,2560]{0,1:T(8,128)(2,1)} %all-gather.5.cloned.1.call-done, bf16[256,896]{1,0:T(8,128)(2,1)S(1)} %get-tuple-element.19, bf16[256,896]{1,0:T(8,128)(2,1)S(1)} %get-tuple-element.18), kind=kOutput, calls=%fused_computation.7 | convolution fusion | flops 2351955968 | bytes 8126464 | tf_op jit(solution)/shard_map/dot_general | solution.py:56
  186.3 1.7 fusion.34
  188.0 0.0 copy-start.6
  188.0 0.0 copy-start.1
  188.0 0.0 all-reduce.8.cloned.1.call-update
  188.0 0.0 reduce-scatter.2.cloned.1.call-start
  188.8 0.0 copy-done.6
  188.9 0.1 select_reduce_fusion
  189.0 86.6 %all-reduce.8.cloned.1.call-done = (bf16[256,2560]{1,0:T(8,128)(2,1)}, bf16[256,2560]{1,0:T(8,128)(2,1)}) async-done(((bf16[256,2560]{1,0:T(8,128)(2,1)}, bf16[256,2560]{1,0:T(8,128)(2,1)}), (bf16[256,2560]{1,0:T(8,128)(2,1)}, bf16[256,2560]{1,0:T(8,128)(2,1)})) %all-reduce.8.cloned.1.call-update) | async-done | bytes 2621456 | tf_op jit(solution)/shard_map/psum | solution.py:65
  275.5 0.0 copy-done.1
  275.5 2.5 fusion.11
  278.1 0.0 copy-start.3
  278.1 0.0 copy-start.4
  278.1 5.3 %fusion.12 = f32[512,896]{1,0:T(8,128)S(1)} fusion(bf16[896,2560]{0,1:T(8,128)(2,1)} %all-gather.5.cloned.1.call-done, bf16[256,2560]{1,0:T(8,128)(2,1)S(1)} %get-tuple-element.21, bf16[256,2560]{1,0:T(8,128)(2,1)S(1)} %get-tuple-element.20), kind=kOutput, calls=%fused_computation.17 | convolution fusion | flops 2354053120 | bytes 9043968 | tf_op jit(solution)/shard_map/dot_general | solution.py:71
  283.4 0.0 copy-start.8
  283.4 0.0 copy-done.3
  283.4 0.0 copy-done.4
  283.4 1.3 multiply_reduce_fusion
  284.7 0.0 copy-done.8
  284.7 3.7 convolution_convert_fusion
  288.4 0.0 copy-start.5
  288.5 0.0 reduce-scatter.2.cloned.1.call-update
  288.5 0.9 copy-done.5
  289.4 0.7 multiply_reduce_fusion.1
  290.0 12.9 %all-reduce.2 = (f32[]{:T(128)}, f32[]{:T(128)}) all-reduce(f32[]{:T(128)} %get-tuple-element.14, f32[]{:T(128)} %multiply_reduce_fusion.1), channel_id=1, replica_groups=mesh['dp_0'=4,'dp_1'=4,'dp_2'=2,'tensor_0'=2,'tensor_1'=4] {'dp_0'}, use_global_device_ids=true, to_apply=%region_6.7 | all-reduce | flops 2 | bytes 16 | tf_op jit(solution)/shard_map/psum | solution.py:23
  302.9 11.1 %all-reduce.1 = (f32[]{:T(128)}, f32[]{:T(128)}) all-reduce(f32[]{:T(128)} %get-tuple-element.6, f32[]{:T(128)} %get-tuple-element.7), channel_id=1, replica_groups=mesh['dp_0'=4,'dp_1'=4,'dp_2'=2,'tensor_0'=2,'tensor_1'=4] {'dp_1'}, use_global_device_ids=true, to_apply=%region_7.8 | all-reduce | flops 2 | bytes 16 | tf_op jit(solution)/shard_map/psum | solution.py:23
  314.0 3.1 all-reduce.4
  317.1 5.5 %all-reduce.3 = (f32[]{:T(128)}, f32[]{:T(128)}) all-reduce(f32[]{:T(128)} %get-tuple-element.10, f32[]{:T(128)} %get-tuple-element.11), channel_id=1, replica_groups=mesh['dp_0'=4,'dp_1'=4,'dp_2'=2,'tensor_0'=2,'tensor_1'=4] {'tensor_0'}, use_global_device_ids=true, to_apply=%region_9.10 | all-reduce | flops 2 | bytes 16 | tf_op jit(solution)/shard_map/psum | solution.py:23
  322.6 9.6 %all-reduce = (f32[]{:T(128)}, f32[]{:T(128)}) all-reduce(f32[]{:T(128)} %get-tuple-element.8, f32[]{:T(128)} %get-tuple-element.9), channel_id=1, replica_groups=mesh['dp_0'=4,'dp_1'=4,'dp_2'=2,'tensor_0'=2,'tensor_1'=4] {'tensor_1'}, use_global_device_ids=true, to_apply=%region_10.11 | all-reduce | flops 2 | bytes 16 | tf_op jit(solution)/shard_map/psum | solution.py:23
  333.5 57.2 %reduce-scatter.2.cloned.1.call-done = bf16[80,896]{1,0:T(8,128)(2,1)} async-done(((bf16[2560,896]{1,0:T(8,128)(2,1)}), bf16[80,896]{1,0:T(8,128)(2,1)}) %reduce-scatter.2.cloned.1.call-update) | async-done | bytes 143376 | tf_op jit(solution)/shard_map/reduce_scatter | solution.py:92
  390.7 1.6 convert_element_type.65
  (3 shorter events, 0.0 us)
Async XLA Ops:
  7.2 101.6 %copy-start = (bf16[256,2560]{1,0:T(8,128)(2,1)S(1)}, bf16[256,2560]{1,0:T(8,128)(2,1)}, u32[]{:S(2)}) copy-start(bf16[256,2560]{1,0:T(8,128)(2,1)} %param.9) | copy-start | bytes 3932164
  7.2 101.6 %copy-start.7 = (f32[2560]{0:T(1024)S(1)}, f32[2560]{0:T(1024)}, u32[]{:S(2)}) copy-start(f32[2560]{0:T(1024)} %param.11) | copy-start | bytes 30724
  7.2 101.5 %all-gather.3.cloned.1.call-start = ((), (), s32[]{:S(2)}) async-start(), calls=%async_computation.1 | async-start | bytes 14192640 | tf_op jit(solution)/shard_map/all_gather | solution.py:14
  9.2 171.3 %all-gather.5.cloned.1.call-start = ((), (), s32[]{:S(2)}) async-start(), calls=%async_computation.2 | async-start | bytes 4730880 | tf_op jit(solution)/shard_map/all_gather | solution.py:55
  9.9 265.6 %all-reduce.8.cloned.1.call-start = ((), (), s32[]{:S(2)}) async-start(), calls=%async_computation.4 | async-start | bytes 5242880 | tf_op jit(solution)/shard_map/psum | solution.py:65
  116.5 0.9 copy-start.2
  188.0 0.8 copy-start.6
  188.0 87.5 %copy-start.1 = (bf16[256,2560]{1,0:T(8,128)(2,1)S(1)}, bf16[256,2560]{1,0:T(8,128)(2,1)}, u32[]{:S(2)}) copy-start(bf16[256,2560]{1,0:T(8,128)(2,1)} %param.10) | copy-start | bytes 3932164
  188.0 202.7 %reduce-scatter.2.cloned.1.call-start = ((), (), s32[]{:S(2)}) async-start(), calls=%async_computation.3 | async-start | bytes 4730880 | tf_op jit(solution)/shard_map/reduce_scatter | solution.py:92
  278.1 5.3 %copy-start.3 = (f32[256,896]{1,0:T(8,128)S(1)}, f32[256,896]{1,0:T(8,128)}, u32[]{:S(2)}) copy-start(f32[256,896]{1,0:T(8,128)} %copy-done.2) | copy-start | bytes 2752516
  278.1 5.3 %copy-start.4 = (f32[256,896]{1,0:T(8,128)S(1)}, f32[256,896]{1,0:T(8,128)}, u32[]{:S(2)}) copy-start(f32[256,896]{1,0:T(8,128)} %get-tuple-element.22) | copy-start | bytes 2752516
  283.4 1.3 copy-start.8
  288.4 0.9 copy-start.5
Sparse Core Ops, SparseCore 0:
  10.6 98.0 all-gather.2
  111.3 69.1 all-gather.4
  188.2 87.3 all-reduce.7
  288.6 102.0 reduce-scatter.1
where the time goes:
time: 401 us; the launch traced here: 400 us
  waiting for transfers between devices  300 us (75%)
  blocking collectives  42.1 us (10%)
  matrix products  27.5 us (7%)
  between operations  17.1 us (4%)
  other arithmetic  9.85 us (2%)
    all_gather x1, waiting for transfers between devices, in_one_piece(): filled, at, outs = (lax.all_gather(both, axis, axis=dim, tiled=True), 0, [])  97.1 us
    psum x1, waiting for transfers between devices, shards(): lax.psum(branch_tan.astype(jnp.bfloat16), TENSOR).astype(jnp.float32)  86.6 us
    all_gather x1, waiting for transfers between devices, shards(): down_full = lax.all_gather(down_weight, DP, axis=1, tiled=True)  58.1 us
    reduce_scatter x1, waiting for transfers between devices, shards(): lax.psum_scatter(lax.optimization_barrier(product.astype(jnp.bfloat16)).a...  57.2 us
    psum x5, blocking collectives, one_axis_at_a_time(): value = lax.psum(value, axis)  42.1 us
    dot_general x3, matrix products, shards(): jnp.dot(columns, piece, preferred_element_type=jnp.float32)  12.7 us
  transfers between devices with their start and end apart: 4, of which 4 were waited for; matrix products, arithmetic and copies ran while one was open for 4% of the time, Pallas kernels for 0%

commit v1 on v0

--- a/solution.py
+++ b/solution.py
@@ -7,6 +7,14 @@
 DP = ("dp_0", "dp_1", "dp_2")
 TENSOR = ("tensor_0", "tensor_1")
 DP_TENSOR = ("dp_0", "dp_1", "dp_2", "tensor_0", "tensor_1")
+
+
+def inputs_produce(x0):
+    block_next = jax.lax.psum(1, axis_name=DP)
+    everything = jax.lax.all_to_all(
+        jnp.stack(block_next * [x0]), axis_name=DP, split_axis=0, concat_axis=0
+    )
+    return jnp.concatenate(everything, axis=1)
 
 
 def in_one_piece(arrays, axis, dim, along):
@@ -52,7 +60,7 @@
     bend = sigma * (1.0 - sigma) * (2.0 + gate_pre * (1.0 - 2.0 * sigma))
     hidden = (gate_pre * sigma * up_pre).astype(jnp.bfloat16)
     hidden_tan = (slope * gate_tan * up_pre).astype(jnp.bfloat16)
-    down_full = lax.all_gather(down_weight, DP, axis=1, tiled=True)
+    down_full = inputs_produce(down_weight)
     stacked = jnp.dot(
         jnp.concatenate([hidden, hidden_tan], axis=0), down_full, preferred_element_type=jnp.float32
     )

time: 401 us -> 435 us (1.085)
  waiting for transfers between devices: 300 us -> 320 us
  starting transfers between devices: 0.16 us -> 12 us
    all_gather x1, waiting for transfers between devices: 97.1 us -> 174 us  [in_one_piece(): filled, at, outs = (lax.all_gather(both, axis, axis=dim, tiled=True), 0, [])]
    all_gather x1 -> x0, waiting for transfers between devices: 58.1 us -> none  [shards(): down_full = lax.all_gather(down_weight, DP, axis=1, tiled=True)]
    all_to_all x0 -> x1, starting transfers between devices: none -> 11.7 us  [inputs_produce(): jax.lax.all_to_all(jnp.stack(block_next * [x0]), axis_name=DP, split_axis...]
  transfers between devices with their start and end apart: 4 -> 4, of which waited for: 4 -> 3; matrix products, arithmetic and copies ran while one was open for 4% -> 4% of each run, Pallas kernels for 0% -> 0%
where the time goes in v1:
time: 435 us; the launch traced here: 434 us
  waiting for transfers between devices  320 us (74%)
  blocking collectives  42.1 us (10%)
  matrix products  27.5 us (6%)
  between operations  17.1 us (4%)
  starting transfers between devices  12 us (3%)
  other arithmetic  8.46 us (2%)
  local copies, waits for them, and re-layouts  6.91 us (2%)
    all_gather x1, waiting for transfers between devices, in_one_piece(): filled, at, outs = (lax.all_gather(both, axis, axis=dim, tiled=True), 0, [])  174 us
    psum x1, waiting for transfers between devices, shards(): lax.psum(branch_tan.astype(jnp.bfloat16), TENSOR).astype(jnp.float32)  88.6 us
    reduce_scatter x1, waiting for transfers between devices, shards(): lax.psum_scatter(lax.optimization_barrier(product.astype(jnp.bfloat16)).a...  57.1 us
    psum x5, blocking collectives, one_axis_at_a_time(): value = lax.psum(value, axis)  42.1 us
    dot_general x3, matrix products, shards(): jnp.dot(columns, piece, preferred_element_type=jnp.float32)  12.7 us
    all_to_all x1, starting transfers between devices, inputs_produce(): jax.lax.all_to_all(jnp.stack(block_next * [x0]), axis_name=DP, split_axis...  11.7 us
  transfers between devices with their start and end apart: 4, of which 3 were waited for; matrix products, arithmetic and copies ran while one was open for 4% of the time, Pallas kernels for 0%

profile of v1, /device:TPU:2, one launch (start us, length us, event | category | flops | bytes accessed | tf_op | source)
XLA Modules:
  0.0 434.2 jit_solution(2164365283169006555)
XLA Ops:
  7.2 0.0 all-gather.2.cloned.1.call-start
  7.2 1.9 pad_maximum_fusion
  9.1 0.0 all-gather.2.cloned.1.call-update
  9.1 3.4 stack.2
  12.5 0.0 copy-start
  12.5 0.0 copy-start.7
  12.5 11.7 %all-to-all-start = ((bf16[32,896,80]{1,2,0:T(8,128)(2,1)}), bf16[32,896,80]{1,2,0:T(8,128)(2,1)}, u32[]{:S(2)}, u32[]{:S(2)}) async-start(bf16[32,896,80]{1,2,0:T(8,128)(2,1)} %stack.2), calls=%async_computation | async-start | bytes 9175040 | tf_op jit(solution)/shard_map/all_to_all | solution.py:14
  24.2 0.0 all-reduce.8.cloned.1.call-start
  24.3 0.0 copy-done
  24.3 0.3 fusion.6
  24.6 174.1 %all-gather.2.cloned.1.call-done = bf16[2560,2688]{1,0:T(8,128)(2,1)} async-done(((bf16[80,2688]{1,0:T(8,128)(2,1)}), bf16[2560,2688]{1,0:T(8,128)(2,1)}) %all-gather.2.cloned.1.call-update) | async-done | bytes 13762576 | tf_op jit(solution)/shard_map/all_gather | solution.py:22
  198.8 0.0 copy-done.7
  198.8 3.9 fusion
  202.7 3.9 fusion.4
  206.5 0.0 copy-start.2
  206.6 0.9 copy-done.2
  207.5 4.9 %multiply_convert_fusion.2 = (bf16[256,896]{1,0:T(8,128)(2,1)S(1)}, bf16[256,896]{1,0:T(8,128)(2,1)S(1)}, f32[256,896]{1,0:T(8,128)}) fusion(f32[256,896]{1,0:T(8,128)S(1)} %fusion.4, f32[256,896]{1,0:T(8,128)S(1)} %fusion, bf16[2560,2688]{1,0:T(8,128)(2,1)} %all-gather.2.cloned.1.call-done, bf16[256,2560]{1,0:T(8,128)(2,1)S(1)} %copy-done, ...), kind=kOutput, calls=%fused_computation.39 | convolution fusion | flops 1180008448 | bytes 9579520 | tf_op jit(solution)/shard_map/dot_general | solution.py:56
  212.4 0.0 all-to-all-done
  212.4 5.8 %convolution_convert_fusion.1 = bf16[512,2560]{1,0:T(8,128)(2,1)S(1)} fusion(bf16[896,2560]{0,1:T(8,128)(2,1)} %bitcast.2, bf16[256,896]{1,0:T(8,128)(2,1)S(1)} %get-tuple-element.19, bf16[256,896]{1,0:T(8,128)(2,1)S(1)} %get-tuple-element.18), kind=kOutput, calls=%fused_computation.7 | convolution fusion | flops 2351955968 | bytes 8126464 | tf_op jit(solution)/shard_map/dot_general | solution.py:64
  218.2 1.7 fusion.34
  219.9 0.0 copy-start.6
  219.9 0.0 copy-start.1
  219.9 0.0 all-reduce.8.cloned.1.call-update
  220.0 0.2 reduce-scatter.2.cloned.1.call-start
  221.0 0.0 copy-done.6
  221.0 0.1 select_reduce_fusion
  221.1 88.6 %all-reduce.8.cloned.1.call-done = (bf16[256,2560]{1,0:T(8,128)(2,1)}, bf16[256,2560]{1,0:T(8,128)(2,1)}) async-done(((bf16[256,2560]{1,0:T(8,128)(2,1)}, bf16[256,2560]{1,0:T(8,128)(2,1)}), (bf16[256,2560]{1,0:T(8,128)(2,1)}, bf16[256,2560]{1,0:T(8,128)(2,1)})) %all-reduce.8.cloned.1.call-update) | async-done | bytes 2621456 | tf_op jit(solution)/shard_map/psum | solution.py:73
  309.8 0.0 copy-done.1
  309.8 2.5 fusion.11
  312.3 0.0 copy-start.3
  312.3 0.0 copy-start.4
  312.3 5.3 %fusion.12 = f32[512,896]{1,0:T(8,128)S(1)} fusion(bf16[896,2560]{0,1:T(8,128)(2,1)} %bitcast.2, bf16[256,2560]{1,0:T(8,128)(2,1)S(1)} %get-tuple-element.21, bf16[256,2560]{1,0:T(8,128)(2,1)S(1)} %get-tuple-element.20), kind=kOutput, calls=%fused_computation.17 | convolution fusion | flops 2354053120 | bytes 9043968 | tf_op jit(solution)/shard_map/dot_general | solution.py:79
  317.6 0.0 copy-start.8
  317.6 0.0 copy-done.3
  317.6 0.0 copy-done.4
  317.6 1.3 multiply_reduce_fusion
  318.9 0.0 copy-done.8
  318.9 3.7 convolution_convert_fusion
  322.7 0.0 copy-start.5
  322.7 0.0 reduce-scatter.2.cloned.1.call-update
  322.7 0.9 copy-done.5
  323.6 0.7 multiply_reduce_fusion.1
  324.3 12.9 %all-reduce.2 = (f32[]{:T(128)}, f32[]{:T(128)}) all-reduce(f32[]{:T(128)} %get-tuple-element.14, f32[]{:T(128)} %multiply_reduce_fusion.1), channel_id=1, replica_groups=mesh['dp_0'=4,'dp_1'=4,'dp_2'=2,'tensor_0'=2,'tensor_1'=4] {'dp_0'}, use_global_device_ids=true, to_apply=%region_6.7 | all-reduce | flops 2 | bytes 16 | tf_op jit(solution)/shard_map/psum | solution.py:31
  337.1 11.1 %all-reduce.1 = (f32[]{:T(128)}, f32[]{:T(128)}) all-reduce(f32[]{:T(128)} %get-tuple-element.6, f32[]{:T(128)} %get-tuple-element.7), channel_id=1, replica_groups=mesh['dp_0'=4,'dp_1'=4,'dp_2'=2,'tensor_0'=2,'tensor_1'=4] {'dp_1'}, use_global_device_ids=true, to_apply=%region_7.8 | all-reduce | flops 2 | bytes 16 | tf_op jit(solution)/shard_map/psum | solution.py:31
  348.2 3.1 all-reduce.4
  351.3 5.5 %all-reduce.3 = (f32[]{:T(128)}, f32[]{:T(128)}) all-reduce(f32[]{:T(128)} %get-tuple-element.10, f32[]{:T(128)} %get-tuple-element.11), channel_id=1, replica_groups=mesh['dp_0'=4,'dp_1'=4,'dp_2'=2,'tensor_0'=2,'tensor_1'=4] {'tensor_0'}, use_global_device_ids=true, to_apply=%region_9.10 | all-reduce | flops 2 | bytes 16 | tf_op jit(solution)/shard_map/psum | solution.py:31
  356.8 9.5 %all-reduce = (f32[]{:T(128)}, f32[]{:T(128)}) all-reduce(f32[]{:T(128)} %get-tuple-element.8, f32[]{:T(128)} %get-tuple-element.9), channel_id=1, replica_groups=mesh['dp_0'=4,'dp_1'=4,'dp_2'=2,'tensor_0'=2,'tensor_1'=4] {'tensor_1'}, use_global_device_ids=true, to_apply=%region_10.11 | all-reduce | flops 2 | bytes 16 | tf_op jit(solution)/shard_map/psum | solution.py:31
  367.7 57.1 %reduce-scatter.2.cloned.1.call-done = bf16[80,896]{1,0:T(8,128)(2,1)} async-done(((bf16[2560,896]{1,0:T(8,128)(2,1)}), bf16[80,896]{1,0:T(8,128)(2,1)}) %reduce-scatter.2.cloned.1.call-update) | async-done | bytes 143376 | tf_op jit(solution)/shard_map/reduce_scatter | solution.py:100
  424.9 1.6 convert_element_type.65
  (3 shorter events, 0.0 us)
Async XLA Ops:
  7.2 191.6 %all-gather.2.cloned.1.call-start = ((), (), s32[]{:S(2)}) async-start(), calls=%async_computation.2 | async-start | bytes 14192640 | tf_op jit(solution)/shard_map/all_gather | solution.py:22
  12.5 11.8 %copy-start = (bf16[256,2560]{1,0:T(8,128)(2,1)S(1)}, bf16[256,2560]{1,0:T(8,128)(2,1)}, u32[]{:S(2)}) copy-start(bf16[256,2560]{1,0:T(8,128)(2,1)} %param.9) | copy-start | bytes 3932164
  12.5 186.3 %copy-start.7 = (f32[2560]{0:T(1024)S(1)}, f32[2560]{0:T(1024)}, u32[]{:S(2)}) copy-start(f32[2560]{0:T(1024)} %param.11) | copy-start | bytes 30724
  12.5 199.9 %all-to-all-start = ((bf16[32,896,80]{1,2,0:T(8,128)(2,1)}), bf16[32,896,80]{1,2,0:T(8,128)(2,1)}, u32[]{:S(2)}, u32[]{:S(2)}) async-start(bf16[32,896,80]{1,2,0:T(8,128)(2,1)} %stack.2), calls=%async_computation | async-start | bytes 9175040 | tf_op jit(solution)/shard_map/all_to_all | solution.py:14
  24.2 285.5 %all-reduce.8.cloned.1.call-start = ((), (), s32[]{:S(2)}) async-start(), calls=%async_computation.4 | async-start | bytes 5242880 | tf_op jit(solution)/shard_map/psum | solution.py:73
  206.5 0.9 copy-start.2
  219.9 1.1 copy-start.6
  219.9 89.8 %copy-start.1 = (bf16[256,2560]{1,0:T(8,128)(2,1)S(1)}, bf16[256,2560]{1,0:T(8,128)(2,1)}, u32[]{:S(2)}) copy-start(bf16[256,2560]{1,0:T(8,128)(2,1)} %param.10) | copy-start | bytes 3932164
  220.0 204.9 %reduce-scatter.2.cloned.1.call-start = ((), (), s32[]{:S(2)}) async-start(), calls=%async_computation.3 | async-start | bytes 4730880 | tf_op jit(solution)/shard_map/reduce_scatter | solution.py:100
  312.3 5.3 %copy-start.3 = (f32[256,896]{1,0:T(8,128)S(1)}, f32[256,896]{1,0:T(8,128)}, u32[]{:S(2)}) copy-start(f32[256,896]{1,0:T(8,128)} %copy-done.2) | copy-start | bytes 2752516
  312.3 5.3 %copy-start.4 = (f32[256,896]{1,0:T(8,128)S(1)}, f32[256,896]{1,0:T(8,128)}, u32[]{:S(2)}) copy-start(f32[256,896]{1,0:T(8,128)} %get-tuple-element.22) | copy-start | bytes 2752516
  317.6 1.3 copy-start.8
  322.7 0.9 copy-start.5
Sparse Core Ops, SparseCore 0:
  10.6 188.1 all-gather.1
  220.1 89.6 all-reduce.7
  322.8 101.9 reduce-scatter.1
